TPU v7x, 32 devices: a whole 2x2x4 slice. The times are simulated.
32 devices in a mesh: rep: 2 (over x), shard: 16 (over z, y, core).
Axes of the slice: x: 2, y: 2, z: 4, core: 2. Of those that a mesh axis runs over, the one named last changes fastest.
Arguments:
- features: float32 [16384, 256], P(('rep', 'shard')), may hold values from -6 to 6
- seed_self: float32 [4096, 256], P(('rep', 'shard')), may hold values from -6 to 6
- hub_ids: int32 [4096], P(('rep', 'shard')), may hold values from 0 to 511
- requests: int32 [512, 32], P(('rep', 'shard')), may hold values from 0 to 511
- counts: int32 [512], P(('rep', 'shard')), may hold values from 1 to 32, as said below
- neighbors: int32 [4096, 15], P(('rep', 'shard')), may hold values from 0 to 767
- weight: float32 [256, 256], replicated, may hold values from -1 to 1
- out_bias: float32 [256], replicated, may hold values from -4 to 4
Outputs:
- embedded: float32 [4096, 256], P(('rep', 'shard'))
Inputs may be any that keep to these rules, and one draw needn't show every extreme that they name: `hub_ids`: offsets into the block of features of the same device. `requests`: row d of a device's lists holds offsets into the block of features of the device at shard index d with the same rep index; empty slots hold offsets too. counts[r, s, d] slots of the list from shard index s to shard index d are live, the first ones; for every rep index some destination has 32 live slots from every source. `neighbors`: A code below 256 names a row of the device's hub cache; a code 256 + d * 32 + c names slot c of the device's list to shard index d, and counts only where that slot is live.
All inputs are finite; a program needn't handle non-finite values.
Results may differ from a plain program's by a relative error of at most 0.0003.
Values sent between devices are 32-bit elements; how exact they have to be, the bound alone decides.
A program may use at most 64 MiB of HBM per device.

v0:
```python
import functools

import jax
import jax.numpy as jnp
from jax import lax
from jax.experimental import pallas as pl
from jax.experimental.pallas import tpu as pltpu
from jax.sharding import PartitionSpec as P

LANES = 128


def halves(values):
    high = values.astype(jnp.bfloat16)
    low = (values - high.astype(jnp.float32)).astype(jnp.bfloat16)
    return high, low


def dot(left, right):
    return jnp.dot(left, right, preferred_element_type=jnp.float32)


def columns_of(rows):
    count = rows.shape[0]
    if count < LANES:
        rows = jnp.concatenate([rows, jnp.zeros((LANES - count, LANES), rows.dtype)], axis=0)
    return rows.T


def kernel(
    n, reps, feat_hbm, self_hbm, hub_ref, req_ref, cnt_ref, nbr_ref, weight_hbm, out_ref,
    feat, own, weight, table, tables, req_recv, gathered, fetched, hubs, slot_tally,
    local_sem, ask_sem, req_recv_sem, table_send_sem, table_recv_sem, row_send_sem, row_recv_sem, hub_send_sem, hub_recv_sem,
):
    me = lax.axis_index("shard")
    rep = lax.axis_index("rep")
    rows, width = feat.shape
    cap = req_ref.shape[1]
    hub_dev = hub_ref.shape[1]
    fanout, seeds = nbr_ref.shape
    hub_total = hub_dev * reps
    quarter = n // 4
    block, place = me // quarter, lax.rem(me, quarter)
    side = block // 2
    inner = lax.rem(block + side, 2)
    is_inner = inner == 1
    near = 1 + lax.rem(block, 2)
    edge = 3 * side
    twin = 3 - block
    far = 3 - edge
    turns = [lax.rem(place + q, quarter) for q in range(quarter)]

    loads = [
        pltpu.make_async_copy(src, dst, local_sem.at[i])
        for i, (src, dst) in enumerate(((feat_hbm, feat), (weight_hbm, weight), (self_hbm, own)))
    ]
    for load in loads:
        load.start()

    barrier = pltpu.get_barrier_semaphore()

    def greet(peer_block, places):
        for spot in places:
            pl.semaphore_signal(barrier, inc=1, device_id={"shard": peer_block * quarter + spot})

    greet(block, turns[1:])
    greet(near, turns)

    @pl.when(is_inner)
    def _():
        greet(edge, turns)

    for off in range(1, reps):
        pl.semaphore_signal(barrier, inc=1, device_id={"rep": lax.rem(rep + off, reps)})

    lists = jnp.concatenate([req_ref[...], jnp.zeros((n, LANES - cap), jnp.int32)], axis=1)
    table[...] = lists.reshape(4, quarter, 1, LANES)
    req_recv[block, place] = table[block, place]
    pl.semaphore_wait(barrier, quarter - 1 + quarter + quarter * inner + reps - 1)

    def row_copies(source, owner_block, to_block, lane, places):
        return [
            pltpu.make_async_remote_copy(
                src_ref=source.at[to_block, spot],
                dst_ref=req_recv.at[owner_block, place],
                send_sem=ask_sem.at[lane, q],
                recv_sem=req_recv_sem.at[owner_block, place],
                device_id={"shard": to_block * quarter + spot},
            )
            for q, spot in enumerate(places)
        ]

    def table_copy(source, to_block, slot, lane):
        return pltpu.make_async_remote_copy(
            src_ref=source,
            dst_ref=tables.at[slot],
            send_sem=table_send_sem.at[lane],
            recv_sem=table_recv_sem.at[slot],
            device_id={"shard": to_block * quarter + place},
        )

    def start(copies):
        for copy in copies:
            copy.start()

    def sent(copies):
        for copy in copies:
            copy.wait_send()

    def table_wait(slot):
        pltpu.make_async_copy(tables.at[slot], tables.at[slot], table_recv_sem.at[slot]).wait()

    asks = row_copies(table, block, near, 0, turns) + row_copies(table, block, block, 1, turns[1:])
    edge_asks = row_copies(table, block, edge, 2, turns)
    own_table = table_copy(table, near, inner, 0)
    passed = [
        row_copies(tables.at[0], edge, twin, 3, turns) + [table_copy(tables.at[0], twin, 2, 1)],
        row_copies(tables.at[1], twin, edge, 4, turns),
        row_copies(tables.at[2], far, edge, 5, turns),
    ]

    own_table.start()
    start(asks)

    @pl.when(is_inner)
    def _():
        start(edge_asks)

    loads[0].wait()
    high, low = halves(feat[...])
    row_iota = lax.broadcasted_iota(jnp.int32, (LANES, rows), 1)

    @pl.when(is_inner)
    def _():
        for slot in (0, 1):
            table_wait(slot)
            start(passed[slot])

    batch = min(LANES // cap, quarter)

    def reply_copy(group, owner_block, q):
        spot = turns[q]
        return pltpu.make_async_remote_copy(
            src_ref=gathered.at[group, spot],
            dst_ref=fetched.at[me],
            send_sem=row_send_sem.at[group, q],
            recv_sem=row_recv_sem.at[me],
            device_id={"shard": owner_block * quarter + spot},
        )

    def unless_own(peer_block, q, action):
        if q:
            action()
        else:
            pl.when(peer_block != block)(action)

    def answer(group, peer_block):
        for q, spot in enumerate(turns):
            ref = req_recv.at[peer_block, spot]
            unless_own(peer_block, q, pltpu.make_async_copy(ref, ref, req_recv_sem.at[peer_block, spot]).wait)
        request_columns = columns_of(req_recv[peer_block].reshape(quarter, LANES))
        for first in range(0, quarter, batch):
            pick = jnp.concatenate(
                [
                    (request_columns[:cap, q : q + 1] == row_iota[:cap]).astype(jnp.float32)
                    for q in range(first, first + batch)
                ],
                axis=0,
            ).astype(jnp.bfloat16)
            picked = dot(pick, high) + dot(pick, low)
            gathered[group, first : first + batch] = picked.reshape(batch, cap, width)
        for q in range(quarter):
            unless_own(peer_block, q, reply_copy(group, peer_block, q).start)

    peer_blocks = (near, edge, 2 - lax.rem(block, 2), far)
    own_group = 1 + inner
    for group in range(3):
        answer(group, peer_blocks[group])

    @pl.when(is_inner)
    def _():
        table_wait(2)
        start(passed[2])

    answer(3, peer_blocks[3])
    fetched[me] = gathered[own_group, place]

    hub_columns = columns_of(jnp.broadcast_to(hub_ref[...], (8, hub_dev)))
    pick = (hub_columns[:, 0:1] == row_iota).astype(jnp.float32).astype(jnp.bfloat16)
    hubs[rep] = dot(pick, high) + dot(pick, low)
    shares = []
    for off in range(1, reps):
        share = pltpu.make_async_remote_copy(
            src_ref=hubs.at[rep],
            dst_ref=hubs.at[rep],
            send_sem=hub_send_sem.at[off],
            recv_sem=hub_recv_sem.at[rep],
            device_id={"rep": lax.rem(rep + off, reps)},
        )
        share.start()
        shares.append(share)

    code_count = hub_total + n * cap
    code_iota = lax.broadcasted_iota(jnp.int32, (seeds, code_count), 1)
    codes = columns_of(nbr_ref[...])
    tally = jnp.zeros((seeds, code_count), jnp.float32)
    for k in range(fanout):
        tally = tally + (codes[:, k : k + 1] == code_iota).astype(jnp.float32)
    spread = (
        lax.broadcasted_iota(jnp.int32, (n, n * cap), 1) // cap
        == lax.broadcasted_iota(jnp.int32, (n, n * cap), 0)
    ).astype(jnp.float32).astype(jnp.bfloat16)
    fill = jnp.broadcast_to(cnt_ref[...].astype(jnp.float32), (8, n)).astype(jnp.bfloat16)
    slot_fill = dot(fill, spread)[0:1]
    slot_iota = (lax.broadcasted_iota(jnp.int32, (1, n * cap), 1) % cap).astype(jnp.float32)
    slot_live = (slot_iota < slot_fill).astype(jnp.float32)
    hub_tally = tally[:, :hub_total]
    live_tally = tally[:, hub_total:] * slot_live
    taken = 1.0 + jnp.sum(hub_tally, axis=1, keepdims=True) + jnp.sum(live_tally, axis=1, keepdims=True)
    scale = 1.0 / taken
    hub_tally = hub_tally.astype(jnp.bfloat16)
    for b in range(4):
        slot_tally[b] = live_tally[:, b * quarter * cap : (b + 1) * quarter * cap].astype(jnp.bfloat16)

    own_table.wait_send()
    sent(asks)

    @pl.when(is_inner)
    def _():
        sent(edge_asks)
        for copies in passed:
            sent(copies)

    loads[2].wait()
    for off in range(1, reps):
        shares[off - 1].wait_send()
        other = lax.rem(rep + off, reps)
        pltpu.make_async_copy(hubs.at[other], hubs.at[other], hub_recv_sem.at[other]).wait()
    hub_high, hub_low = halves(hubs[...].reshape(hub_total, width))
    total = own[...] + (dot(hub_tally, hub_high) + dot(hub_tally, hub_low))
    loads[1].wait()
    weight_high, weight_low = halves(weight[...])

    for owner_block in (block, block + 1 - 2 * lax.rem(block, 2), 2 - side, far):
        for q, spot in enumerate(turns):
            ref = fetched.at[owner_block * quarter + spot]
            unless_own(owner_block, q, pltpu.make_async_copy(ref, ref, row_recv_sem.at[owner_block * quarter + spot]).wait)
        row_high, row_low = halves(fetched[pl.ds(owner_block * quarter, quarter)].reshape(quarter * cap, width))
        counted = slot_tally[owner_block]
        total = total + (dot(counted, row_high) + dot(counted, row_low))
    mean_high, mean_low = halves(total * scale)
    out_ref[...] = dot(mean_high, weight_high) + (dot(mean_high, weight_low) + dot(mean_low, weight_high))
    for group in range(4):
        for q in range(quarter):
            unless_own(peer_blocks[group], q, reply_copy(group, peer_blocks[group], q).wait_send)


def local(n, reps, features, seed_self, hub_ids, requests, counts, neighbors, weight, out_bias):
    rows, width = features.shape
    cap = requests.shape[1]
    hub_dev = hub_ids.shape[0]
    seeds = neighbors.shape[0]
    hbm = pl.BlockSpec(memory_space=pltpu.HBM)
    vmem = pl.BlockSpec(memory_space=pltpu.VMEM)
    dma = pltpu.SemaphoreType.DMA
    product = pl.pallas_call(
        functools.partial(kernel, n, reps),
        out_shape=jax.ShapeDtypeStruct((seeds, width), jnp.float32),
        in_specs=[hbm, hbm, vmem, vmem, vmem, vmem, hbm],
        out_specs=vmem,
        scratch_shapes=[
            pltpu.VMEM((rows, width), jnp.float32),
            pltpu.VMEM((seeds, width), jnp.float32),
            pltpu.VMEM(weight.shape, jnp.float32),
            pltpu.VMEM((4, n // 4, 1, LANES), jnp.int32),
            pltpu.VMEM((3, 4, n // 4, 1, LANES), jnp.int32),
            pltpu.VMEM((4, n // 4, 1, LANES), jnp.int32),
            pltpu.VMEM((4, n // 4, cap, width), jnp.float32),
            pltpu.VMEM((n, cap, width), jnp.float32),
            pltpu.VMEM((reps, hub_dev, width), jnp.float32),
            pltpu.VMEM((4, seeds, n // 4 * cap), jnp.bfloat16),
            dma((3,)),
            dma((6, n // 4)),
            dma((4, n // 4)),
            dma((2,)),
            dma((3,)),
            dma((4, n // 4)),
            dma((n,)),
            dma((reps,)),
            dma((reps,)),
        ],
        compiler_params=pltpu.CompilerParams(collective_id=0, has_side_effects=True),
    )(features, seed_self, hub_ids[None], requests, counts[None], neighbors.T, weight)
    return jnp.maximum(product + out_bias, 0.0)


def solution(mesh):
    return jax.shard_map(
        functools.partial(local, mesh.shape["shard"], mesh.shape["rep"]),
        mesh=mesh,
        in_specs=(
            P(("rep", "shard"), None),
            P(("rep", "shard"), None),
            P(("rep", "shard")),
            P(("rep", "shard"), None),
            P(("rep", "shard")),
            P(("rep", "shard"), None),
            P(),
            P(),
        ),
        out_specs=P(("rep", "shard"), None),
        check_vma=False,
    )
```

profile of v0, /device:TPU:0, one launch (start us, length us, event | category | flops | bytes accessed | tf_op | source)
XLA Modules:
  0.0 25.9 jit_solution(9593564509565567492)
XLA Ops:
  0.0 0.0 copy-start
  0.0 24.3 %shard_map.82 = f32[128,256]{1,0:T(8,128)} custom-call(f32[512,256]{1,0:T(8,128)} %feat_hbm.1, f32[128,256]{1,0:T(8,128)} %self_hbm.1, s32[1,128]{1,0:T(1,128)} %bitcast.4, s32[16,32]{1,0:T(8,128)} %req_ref.1, s32[1,16]{1,0:T(1,128)} %bitcast.5, s32[15,128]{1,0:T(8,128)} %bitcast.3, f32[256,256]{1,0:T(8,128)} %weight_hbm.1), custom_call_target="tpu_custom_call" | custom-call | tf_op jit(solution)/shard_map/pallas_call | solution.py:266
  24.3 0.0 copy-done
  24.4 1.6 %add_maximum_fusion = f32[128,256]{1,0:T(8,128)} fusion(f32[128,256]{1,0:T(8,128)} %shard_map.82, f32[256]{0:T(256)S(1)} %copy-done), kind=kLoop, calls=%fused_computation | loop fusion | flops 65536 | bytes 263168 | tf_op jit(solution)/shard_map/max | solution.py:294
Async XLA Ops:
  0.0 24.3 %copy-start = (f32[256]{0:T(256)S(1)}, f32[256]{0:T(256)}, u32[]{:S(2)}) copy-start(f32[256]{0:T(256)} %param.15) | copy-start | bytes 3076
where the time goes:
time: 26.1 us; the launch traced here: 25.9 us
  Pallas kernels  24.3 us (93%)
  other arithmetic  1.57 us (6%)
    pallas_call x1, Pallas kernels, local(): pl.pallas_call(functools.partial(kernel, n, reps), out_shape=jax.ShapeDty...  24.3 us
    max x1, other arithmetic, local(): return jnp.maximum(product + out_bias, 0.0)  1.57 us

commit v1 on v0

v1 whole, which is shorter than its diff:
```python
import functools

import jax
import jax.numpy as jnp
from jax import lax
from jax.experimental import pallas as pl
from jax.experimental.pallas import tpu as pltpu
from jax.sharding import PartitionSpec as P

LANES = 128


def halves(values):
    high = values.astype(jnp.bfloat16)
    low = (values - high.astype(jnp.float32)).astype(jnp.bfloat16)
    return high, low


def dot(left, right):
    return jnp.dot(left, right, preferred_element_type=jnp.float32)


def columns_of(rows):
    count = rows.shape[0]
    if count < LANES:
        rows = jnp.concatenate([rows, jnp.zeros((LANES - count, LANES), rows.dtype)], axis=0)
    return rows.T


def kernel(
    n, reps, feat_hbm, self_hbm, hub_hbm, req_hbm, cnt_hbm, nbr_hbm, weight_hbm, out_ref,
    feat, own, weight, hub_ref, req_ref, cnt_ref, nbr_ref, table, req_recv, gathered, fetched, hubs, slot_tally,
    local_sem, ask_sem, ask_recv_sem, row_send_sem, row_recv_sem, hub_send_sem, hub_recv_sem, known,
):
    me = lax.axis_index("shard")
    rep = lax.axis_index("rep")
    rows, width = feat.shape
    cap = req_ref.shape[1]
    hub_dev = hub_ref.shape[1]
    fanout, seeds = nbr_ref.shape
    hub_total = hub_dev * reps
    quarter = n // 4
    block, place = me // quarter, lax.rem(me, quarter)
    side = block // 2
    inner = lax.rem(block + side, 2)
    is_inner = inner == 1
    near = 1 + lax.rem(block, 2)
    edge = 3 * side
    third = 2 - lax.rem(block, 2)
    far = 3 - edge
    turns = [lax.rem(place + q, quarter) for q in range(quarter)]

    loads = [
        pltpu.make_async_copy(src, dst, local_sem.at[i])
        for i, (src, dst) in enumerate(
            (
                (req_hbm, req_ref),
                (feat_hbm, feat),
                (hub_hbm, hub_ref),
                (nbr_hbm, nbr_ref),
                (cnt_hbm, cnt_ref),
                (self_hbm, own),
                (weight_hbm, weight),
            )
        )
    ]
    for load in loads:
        load.start()

    barrier = pltpu.get_barrier_semaphore()

    def greet(peer_block, places):
        for spot in places:
            pl.semaphore_signal(barrier, inc=1, device_id={"shard": peer_block * quarter + spot})

    greet(near, turns)

    @pl.when(is_inner)
    def _():
        greet(edge, turns)

    greet(block, turns[1:])
    for off in range(1, reps):
        pl.semaphore_signal(barrier, inc=1, device_id={"rep": lax.rem(rep + off, reps)})

    loads[0].wait()
    lists = jnp.concatenate([req_ref[...], jnp.zeros((n, LANES - cap), jnp.int32)], axis=1)
    table[...] = lists.reshape(4, quarter, 1, LANES)
    req_recv[block, place] = table[block, place]

    loads[1].wait()
    high, low = halves(feat[...])
    row_iota = lax.broadcasted_iota(jnp.int32, (LANES, rows), 1)

    loads[2].wait()
    hub_columns = columns_of(jnp.broadcast_to(hub_ref[...], (8, hub_dev)))
    pick = (hub_columns[:, 0:1] == row_iota).astype(jnp.float32).astype(jnp.bfloat16)
    hubs[rep] = dot(pick, high) + dot(pick, low)

    pl.semaphore_wait(barrier, quarter - 1 + quarter + quarter * inner + reps - 1)

    def asks(to_block, places):
        return [
            pltpu.make_async_remote_copy(
                src_ref=table.at[to_block, spot],
                dst_ref=req_recv.at[block, place],
                send_sem=ask_sem.at[to_block, spot],
                recv_sem=ask_recv_sem.at[block, place],
                device_id={"shard": to_block * quarter + spot},
            )
            for spot in places
        ]

    def start(copies):
        for copy in copies:
            copy.start()

    def sent(copies):
        for copy in copies:
            copy.wait_send()

    near_asks = asks(near, turns)
    own_asks = asks(block, turns[1:])
    edge_asks = asks(edge, turns)
    far_asks = asks(far, turns)
    two_asks = asks(third, turns)

    def tell(to_block, slot):
        pl.semaphore_signal(known.at[slot], inc=1, device_id={"shard": to_block * quarter + place})

    start(near_asks)

    @pl.when(is_inner)
    def _():
        tell(edge, 0)
        tell(near, 0)
        start(edge_asks)

    start(own_asks)
    shares = []
    for off in range(1, reps):
        share = pltpu.make_async_remote_copy(
            src_ref=hubs.at[rep],
            dst_ref=hubs.at[rep],
            send_sem=hub_send_sem.at[off],
            recv_sem=hub_recv_sem.at[rep],
            device_id={"rep": lax.rem(rep + off, reps)},
        )
        share.start()
        shares.append(share)
    pl.semaphore_wait(known.at[0], 1)

    @pl.when(is_inner)
    def _():
        tell(edge, 1)
        start(far_asks)

    @pl.when(jnp.logical_not(is_inner))
    def _():
        start(two_asks)
        pl.semaphore_wait(known.at[1], 1)
        start(far_asks)

    batch = min(LANES // cap, quarter)

    def reply_copy(owner_block, spot):
        return pltpu.make_async_remote_copy(
            src_ref=gathered.at[owner_block, spot],
            dst_ref=fetched.at[me],
            send_sem=row_send_sem.at[owner_block, spot],
            recv_sem=row_recv_sem.at[me],
            device_id={"shard": owner_block * quarter + spot},
        )

    def answer(peer_block, places, may_own):
        places = list(places)

        def unless_me(spot, action):
            if may_own:
                pl.when((peer_block != block) | (spot != place))(action)
            else:
                action()

        for spot in places:
            ref = req_recv.at[peer_block, spot]
            unless_me(spot, pltpu.make_async_copy(ref, ref, ask_recv_sem.at[peer_block, spot]).wait)
        request_columns = columns_of(jnp.concatenate([req_recv[peer_block, spot] for spot in places], axis=0))
        for first in range(0, len(places), batch):
            group = places[first : first + batch]
            pick = jnp.concatenate(
                [
                    (request_columns[:cap, i : i + 1] == row_iota[:cap]).astype(jnp.float32)
                    for i in range(first, first + len(group))
                ],
                axis=0,
            ).astype(jnp.bfloat16)
            picked = dot(pick, high) + dot(pick, low)
            for i, q in enumerate(group):
                gathered[peer_block, q] = picked[i * cap : (i + 1) * cap]
        for spot in places:
            unless_me(spot, reply_copy(peer_block, spot).start)

    odd, even, every = range(1, quarter, 2), range(0, quarter, 2), range(quarter)
    @pl.when(is_inner)
    def _():
        answer(near, odd, False)
        answer(far, every, False)
        answer(near, even, False)
        answer(edge, every, False)
        answer(block, every, True)

    @pl.when(jnp.logical_not(is_inner))
    def _():
        answer(near, every, False)
        answer(block, every, True)
        answer(third, every, False)
        answer(far, every, False)

    fetched[me] = gathered[block, place]

    loads[3].wait()
    loads[4].wait()
    code_count = hub_total + n * cap
    code_iota = lax.broadcasted_iota(jnp.int32, (seeds, code_count), 1)
    codes = columns_of(nbr_ref[...])
    tally = jnp.zeros((seeds, code_count), jnp.float32)
    for k in range(fanout):
        tally = tally + (codes[:, k : k + 1] == code_iota).astype(jnp.float32)
    spread = (
        lax.broadcasted_iota(jnp.int32, (n, n * cap), 1) // cap
        == lax.broadcasted_iota(jnp.int32, (n, n * cap), 0)
    ).astype(jnp.float32).astype(jnp.bfloat16)
    fill = jnp.broadcast_to(cnt_ref[...].astype(jnp.float32), (8, n)).astype(jnp.bfloat16)
    slot_fill = dot(fill, spread)[0:1]
    slot_iota = (lax.broadcasted_iota(jnp.int32, (1, n * cap), 1) % cap).astype(jnp.float32)
    slot_live = (slot_iota < slot_fill).astype(jnp.float32)
    hub_tally = tally[:, :hub_total]
    live_tally = tally[:, hub_total:] * slot_live
    taken = 1.0 + jnp.sum(hub_tally, axis=1, keepdims=True) + jnp.sum(live_tally, axis=1, keepdims=True)
    scale = 1.0 / taken
    hub_tally = hub_tally.astype(jnp.bfloat16)
    for b in range(4):
        slot_tally[b] = live_tally[:, b * quarter * cap : (b + 1) * quarter * cap].astype(jnp.bfloat16)

    sent(near_asks + own_asks + far_asks)

    @pl.when(is_inner)
    def _():
        sent(edge_asks)

    @pl.when(jnp.logical_not(is_inner))
    def _():
        sent(two_asks)

    loads[5].wait()
    for off in range(1, reps):
        shares[off - 1].wait_send()
        other = lax.rem(rep + off, reps)
        pltpu.make_async_copy(hubs.at[other], hubs.at[other], hub_recv_sem.at[other]).wait()
    hub_high, hub_low = halves(hubs[...].reshape(hub_total, width))
    total = own[...] + (dot(hub_tally, hub_high) + dot(hub_tally, hub_low))
    loads[6].wait()
    weight_high, weight_low = halves(weight[...])

    for owner_block in (block, block + 1 - 2 * lax.rem(block, 2), 2 - side, far):
        for q, spot in enumerate(turns):
            ref = fetched.at[owner_block * quarter + spot]
            arrival = pltpu.make_async_copy(ref, ref, row_recv_sem.at[owner_block * quarter + spot])
            if q:
                arrival.wait()
            else:
                pl.when(owner_block != block)(arrival.wait)
        row_high, row_low = halves(fetched[pl.ds(owner_block * quarter, quarter)].reshape(quarter * cap, width))
        counted = slot_tally[owner_block]
        total = total + (dot(counted, row_high) + dot(counted, row_low))
    mean_high, mean_low = halves(total * scale)
    out_ref[...] = dot(mean_high, weight_high) + (dot(mean_high, weight_low) + dot(mean_low, weight_high))
    for peer_block in (near, edge, third, far):
        for q, spot in enumerate(turns):
            done = reply_copy(peer_block, spot).wait_send
            if q:
                done()
            else:
                pl.when(peer_block != block)(done)


def local(n, reps, features, seed_self, hub_ids, requests, counts, neighbors, weight, out_bias):
    rows, width = features.shape
    cap = requests.shape[1]
    hub_dev = hub_ids.shape[0]
    seeds, fanout = neighbors.shape
    quarter = n // 4
    hbm = pl.BlockSpec(memory_space=pltpu.HBM)
    dma = pltpu.SemaphoreType.DMA
    product = pl.pallas_call(
        functools.partial(kernel, n, reps),
        out_shape=pltpu.VMEM((seeds, width), jnp.float32),
        in_specs=[hbm] * 7,
        out_specs=pl.BlockSpec(memory_space=pltpu.VMEM),
        scratch_shapes=[
            pltpu.VMEM((rows, width), jnp.float32),
            pltpu.VMEM((seeds, width), jnp.float32),
            pltpu.VMEM(weight.shape, jnp.float32),
            pltpu.VMEM((1, hub_dev), jnp.int32),
            pltpu.VMEM((n, cap), jnp.int32),
            pltpu.VMEM((1, n), jnp.int32),
            pltpu.VMEM((fanout, seeds), jnp.int32),
            pltpu.VMEM((4, quarter, 1, LANES), jnp.int32),
            pltpu.VMEM((4, quarter, 1, LANES), jnp.int32),
            pltpu.VMEM((4, quarter, cap, width), jnp.float32),
            pltpu.VMEM((n, cap, width), jnp.float32),
            pltpu.VMEM((reps, hub_dev, width), jnp.float32),
            pltpu.VMEM((4, seeds, quarter * cap), jnp.bfloat16),
            dma((7,)),
            dma((4, quarter)),
            dma((4, quarter)),
            dma((4, quarter)),
            dma((n,)),
            dma((reps,)),
            dma((reps,)),
            pltpu.SemaphoreType.REGULAR((2,)),
        ],
        compiler_params=pltpu.CompilerParams(collective_id=0, has_side_effects=True),
    )(features, seed_self, hub_ids[None], requests, counts[None], neighbors.T, weight)
    return jnp.maximum(product + out_bias, 0.0)


def solution(mesh):
    return jax.shard_map(
        functools.partial(local, mesh.shape["shard"], mesh.shape["rep"]),
        mesh=mesh,
        in_specs=(
            P(("rep", "shard"), None),
            P(("rep", "shard"), None),
            P(("rep", "shard")),
            P(("rep", "shard"), None),
            P(("rep", "shard")),
            P(("rep", "shard"), None),
            P(),
            P(),
        ),
        out_specs=P(("rep", "shard"), None),
        check_vma=False,
    )
```

time: 26.1 us -> 21.2 us (0.81)
  the two profiles are of different devices: /device:TPU:0 before, /device:TPU:16 now
where the time goes in v1:
time: 21.2 us; the launch traced here: 21 us
  Pallas kernels  20.4 us (96%)
  other arithmetic  0.67 us (3%)
    pallas_call x1, Pallas kernels, local(): pl.pallas_call(functools.partial(kernel, n, reps), out_shape=pltpu.VMEM((...  20.4 us
    max x1, other arithmetic, local(): return jnp.maximum(product + out_bias, 0.0)  0.67 us

profile of v1, /device:TPU:16, one launch (start us, length us, event | category | flops | bytes accessed | tf_op | source)
XLA Modules:
  0.0 21.0 jit_solution(9512049297791483737)
XLA Ops:
  0.0 0.0 copy-start
  0.0 20.4 %shard_map.82 = f32[128,256]{1,0:T(8,128)S(1)} custom-call(f32[512,256]{1,0:T(8,128)} %feat_hbm.1, f32[128,256]{1,0:T(8,128)} %self_hbm.1, s32[1,128]{1,0:T(1,128)} %bitcast.4, s32[16,32]{1,0:T(8,128)} %req_hbm.1, s32[1,16]{1,0:T(1,128)} %bitcast.5, s32[15,128]{1,0:T(8,128)} %bitcast.3, f32[256,256]{1,0:T(8,128)} %weight_hbm.1), custom_call_target="tpu_custom_call" | custom-call | tf_op jit(solution)/shard_map/pallas_call | solution.py:295
  20.4 0.0 copy-done
  20.4 0.7 %add_maximum_fusion = f32[128,256]{1,0:T(8,128)} fusion(f32[128,256]{1,0:T(8,128)S(1)} %shard_map.82, f32[256]{0:T(256)S(1)} %copy-done), kind=kLoop, calls=%fused_computation | loop fusion | flops 65536 | bytes 263168 | tf_op jit(solution)/shard_map/max | solution.py:325
Async XLA Ops:
  0.0 20.4 %copy-start = (f32[256]{0:T(256)S(1)}, f32[256]{0:T(256)}, u32[]{:S(2)}) copy-start(f32[256]{0:T(256)} %param.15) | copy-start | bytes 3076

commit v2 on v1

v2 whole, which is shorter than its diff:
```python
import functools

import jax
import jax.numpy as jnp
from jax import lax
from jax.experimental import pallas as pl
from jax.experimental.pallas import tpu as pltpu
from jax.sharding import PartitionSpec as P

LANES = 128
CLIENT, POOL, FEED = 1, 2, 3


def pooled(peer, quarter):
    return peer // quarter == CLIENT and peer % 2 == 0


def halves(values):
    high = values.astype(jnp.bfloat16)
    low = (values - high.astype(jnp.float32)).astype(jnp.bfloat16)
    return high, low


def dot(left, right):
    return jnp.dot(left, right, preferred_element_type=jnp.float32)


def columns_of(rows):
    count = rows.shape[0]
    if count < LANES:
        rows = jnp.concatenate([rows, jnp.zeros((LANES - count, LANES), rows.dtype)], axis=0)
    return rows.T


def kernel(
    n, reps, feat_hbm, self_hbm, hub_hbm, req_hbm, cnt_hbm, nbr_hbm, weight_hbm, out_ref,
    feat, own, weight, hub_ref, req_ref, cnt_ref, nbr_ref, table, req_recv, gathered, fetched, hubs, slot_tally,
    pool, pool_codes, pool_counts, partial, partial_in,
    local_sem, ask_sem, ask_recv_sem, row_send_sem, row_recv_sem, hub_send_sem, hub_recv_sem, present, rep_present,
    pool_sem, code_send_sem, code_recv_sem, partial_sem,
):
    me = lax.axis_index("shard")
    rep = lax.axis_index("rep")
    rows, width = feat.shape
    cap = req_ref.shape[1]
    hub_dev = hub_ref.shape[1]
    fanout, seeds = nbr_ref.shape
    hub_total = hub_dev * reps
    quarter = n // 4
    block, place = me // quarter, lax.rem(me, quarter)

    loads = [
        pltpu.make_async_copy(src, dst, local_sem.at[i])
        for i, (src, dst) in enumerate(
            (
                (req_hbm, req_ref),
                (feat_hbm, feat),
                (hub_hbm, hub_ref),
                (nbr_hbm, nbr_ref),
                (cnt_hbm, cnt_ref),
                (self_hbm, own),
                (weight_hbm, weight),
            )
        )
    ]
    for load in loads:
        load.start()

    barrier = pltpu.get_barrier_semaphore()

    def greet(peer, carry):
        pl.semaphore_signal(barrier, inc=1, device_id={"shard": peer})
        return carry

    lax.fori_loop(me + 1, n, greet, 0)
    for other in range(1, reps):

        @pl.when(other > rep)
        def _():
            pl.semaphore_signal(barrier, inc=1, device_id={"rep": other})

    @pl.when(me + rep > 0)
    def _():
        pl.semaphore_wait(barrier, me + rep)

    def tell(peer, carry):
        pl.semaphore_signal(present.at[me], inc=1, device_id={"shard": peer})
        return carry

    lax.fori_loop(0, me, tell, 0)
    for other in range(reps - 1):

        @pl.when(other < rep)
        def _():
            pl.semaphore_signal(rep_present.at[rep], inc=1, device_id={"rep": other})

    loads[0].wait()
    lists = jnp.concatenate([req_ref[...], jnp.zeros((n, LANES - cap), jnp.int32)], axis=1)
    table[...] = lists.reshape(n, 1, LANES)
    req_recv[me] = table[me]

    loads[3].wait()
    loads[4].wait()

    def ask_copy(peer):
        return pltpu.make_async_remote_copy(
            src_ref=table.at[peer],
            dst_ref=req_recv.at[me],
            send_sem=ask_sem.at[peer],
            recv_sem=ask_recv_sem.at[me],
            device_id={"shard": peer},
        )

    def ask(own_block, to_block):
        for spot in (*range(1, quarter, 2), *range(0, quarter, 2)):
            peer = to_block * quarter + spot
            if to_block > own_block:
                pl.semaphore_wait(present.at[peer], 1)
            if to_block != own_block:
                ask_copy(peer).start()
                continue

            @pl.when(spot > place)
            def _():
                pl.semaphore_wait(present.at[peer], 1)

            @pl.when(spot != place)
            def _():
                ask_copy(peer).start()

    def code_copies():
        peer = POOL * quarter + place
        return [
            pltpu.make_async_remote_copy(
                src_ref=src,
                dst_ref=dst,
                send_sem=code_send_sem.at[i],
                recv_sem=code_recv_sem.at[i],
                device_id={"shard": peer},
            )
            for i, (src, dst) in enumerate(((nbr_ref, pool_codes), (cnt_ref, pool_counts)))
        ]

    def send_codes():
        for copy in code_copies():
            copy.start()

    for b in range(1, 4):

        @pl.when(block == b)
        def _():
            for to_block in range(b):
                ask(b, to_block)

    loads[1].wait()
    high, low = halves(feat[...])
    row_iota = lax.broadcasted_iota(jnp.int32, (LANES, rows), 1)

    loads[2].wait()
    hub_columns = columns_of(jnp.broadcast_to(hub_ref[...], (8, hub_dev)))
    pick = (hub_columns[:, 0:1] == row_iota).astype(jnp.float32).astype(jnp.bfloat16)
    hubs[rep] = dot(pick, high) + dot(pick, low)

    def share_copy(other):
        return pltpu.make_async_remote_copy(
            src_ref=hubs.at[rep],
            dst_ref=hubs.at[rep],
            send_sem=hub_send_sem.at[other],
            recv_sem=hub_recv_sem.at[rep],
            device_id={"rep": other},
        )

    def share():
        for other in range(reps):

            @pl.when(other > rep)
            def _():
                pl.semaphore_wait(rep_present.at[other], 1)

            @pl.when(other != rep)
            def _():
                share_copy(other).start()

    batch = min(LANES // cap, quarter)

    def reply_copy(peer):
        return pltpu.make_async_remote_copy(
            src_ref=gathered.at[peer],
            dst_ref=fetched.at[me],
            send_sem=row_send_sem.at[peer],
            recv_sem=row_recv_sem.at[me],
            device_id={"shard": peer},
        )

    def answer(own_block, peer_block, places):
        peers = [peer_block * quarter + spot for spot in places]

        def unless_me(peer, action):
            if peer_block == own_block:
                pl.when(peer != me)(action)
            else:
                action()

        for peer in peers:
            ref = req_recv.at[peer]
            unless_me(peer, pltpu.make_async_copy(ref, ref, ask_recv_sem.at[peer]).wait)
        request_columns = columns_of(jnp.concatenate([req_recv[peer] for peer in peers], axis=0))
        for first in range(0, len(peers), batch):
            group = peers[first : first + batch]
            pick = jnp.concatenate(
                [
                    (request_columns[:cap, i : i + 1] == row_iota[:cap]).astype(jnp.float32)
                    for i in range(first, first + len(group))
                ],
                axis=0,
            ).astype(jnp.bfloat16)
            picked = dot(pick, high) + dot(pick, low)
            for i, peer in enumerate(group):
                gathered[peer] = picked[i * cap : (i + 1) * cap]
            for peer in group:
                if own_block in (POOL, FEED) and pooled(peer, quarter):
                    row = place + (quarter if own_block == FEED else 0)
                    forward = pltpu.make_async_remote_copy(
                        src_ref=gathered.at[peer],
                        dst_ref=pool.at[row],
                        send_sem=row_send_sem.at[peer],
                        recv_sem=pool_sem.at[row],
                        device_id={"shard": peer + (POOL - CLIENT) * quarter},
                    )
                    if own_block == POOL:
                        pl.when(peer + (POOL - CLIENT) * quarter != me)(forward.start)
                    else:
                        forward.start()
                else:
                    unless_me(peer, reply_copy(peer).start)

    def tally_of(codes, low, count):
        code_iota = low + lax.broadcasted_iota(jnp.int32, (seeds, count), 1)
        tally = jnp.zeros((seeds, count), jnp.float32)
        for k in range(fanout):
            tally = tally + (codes[:, k : k + 1] == code_iota).astype(jnp.float32)
        return tally

    def live_of(counts, low, count):
        spread = (
            low // cap + lax.broadcasted_iota(jnp.int32, (n, count), 1) // cap
            == lax.broadcasted_iota(jnp.int32, (n, count), 0)
        ).astype(jnp.float32).astype(jnp.bfloat16)
        fill = jnp.broadcast_to(counts.astype(jnp.float32), (8, n)).astype(jnp.bfloat16)
        slot_iota = (lax.broadcasted_iota(jnp.int32, (1, count), 1) % cap).astype(jnp.float32)
        return (slot_iota < dot(fill, spread)[0:1]).astype(jnp.float32)

    partial_copy = pltpu.make_async_remote_copy(
        src_ref=partial,
        dst_ref=partial_in,
        send_sem=partial_sem.at[0],
        recv_sem=partial_sem.at[1],
        device_id={"shard": CLIENT * quarter + place},
    )

    def pool_rows():
        for i, ref in enumerate((pool_codes, pool_counts)):
            pltpu.make_async_copy(ref, ref, code_recv_sem.at[i]).wait()
        low = POOL * quarter * cap
        part = quarter * cap
        counted = tally_of(columns_of(pool_codes[...]), hub_total + low, 2 * part)
        counted = (counted * live_of(pool_counts[...], low, 2 * part)).astype(jnp.bfloat16)
        pool[place] = gathered[CLIENT * quarter + place]
        total = None
        for i in range(2):
            for spot in range(quarter):
                row = i * quarter + spot
                arrival = pltpu.make_async_copy(pool.at[row], pool.at[row], pool_sem.at[row])
                if i == 0:
                    pl.when(spot != place)(arrival.wait)
                else:
                    arrival.wait()
            row_high, row_low = halves(pool[i * quarter : (i + 1) * quarter].reshape(part, width))
            chosen = counted[:, i * part : (i + 1) * part]
            term = dot(chosen, row_high) + dot(chosen, row_low)
            total = term if total is None else total + term
        partial[...] = total
        partial_copy.start()

    every, odd, even = range(quarter), range(1, quarter, 2), range(0, quarter, 2)
    front, back = range(quarter // 2), range(quarter // 2, quarter)
    @pl.when(block == 0)
    def _():
        ask(0, 0)
        ask(0, 1)
        ask(0, 2)
        ask(0, 3)
        share()
        answer(0, 1, odd)
        answer(0, 0, every)
        answer(0, 1, even)
        answer(0, 2, every)
        answer(0, 3, every)

    @pl.when(block == 1)
    def _():
        share()
        ask(1, 1)
        ask(1, 2)
        pl.when(lax.rem(me, 2) == 0)(send_codes)
        ask(1, 3)
        answer(1, 2, odd)
        answer(1, 0, every)
        answer(1, 2, even)
        answer(1, 3, every)
        answer(1, 1, every)

    @pl.when(block == 2)
    def _():
        ask(2, 2)
        ask(2, 3)
        share()
        answer(2, 1, odd)
        answer(2, 1, even)
        answer(2, 0, every)
        answer(2, 2, every)
        answer(2, 3, every)
        pl.when(lax.rem(me, 2) == 0)(pool_rows)

    @pl.when(block == 3)
    def _():
        share()
        ask(3, 3)
        answer(3, 3, every)
        answer(3, 1, even)
        answer(3, 2, odd)
        answer(3, 0, every)
        answer(3, 1, odd)
        answer(3, 2, even)

    fetched[me] = gathered[me]

    tally = tally_of(columns_of(nbr_ref[...]), 0, hub_total + n * cap)
    slot_live = live_of(cnt_ref[...], 0, n * cap)
    hub_tally = tally[:, :hub_total]
    live_tally = tally[:, hub_total:] * slot_live
    taken = 1.0 + jnp.sum(hub_tally, axis=1, keepdims=True) + jnp.sum(live_tally, axis=1, keepdims=True)
    scale = 1.0 / taken
    hub_tally = hub_tally.astype(jnp.bfloat16)
    for b in range(4):
        slot_tally[b] = live_tally[:, b * quarter * cap : (b + 1) * quarter * cap].astype(jnp.bfloat16)

    loads[5].wait()
    for other in range(reps):

        @pl.when(other != rep)
        def _():
            pltpu.make_async_copy(hubs.at[other], hubs.at[other], hub_recv_sem.at[other]).wait()

    hub_high, hub_low = halves(hubs[...].reshape(hub_total, width))
    total = own[...] + (dot(hub_tally, hub_high) + dot(hub_tally, hub_low))
    loads[6].wait()
    weight_high, weight_low = halves(weight[...])

    def add_rows(total, owner_block):
        for spot in range(quarter):
            owner = owner_block * quarter + spot

            @pl.when(owner != me)
            def _():
                pltpu.make_async_copy(fetched.at[owner], fetched.at[owner], row_recv_sem.at[owner]).wait()

        row_high, row_low = halves(fetched[pl.ds(owner_block * quarter, quarter)].reshape(quarter * cap, width))
        counted = slot_tally[owner_block]
        return total + (dot(counted, row_high) + dot(counted, row_low))

    def project(total):
        mean_high, mean_low = halves(total * scale)
        out_ref[...] = dot(mean_high, weight_high) + (dot(mean_high, weight_low) + dot(mean_low, weight_high))

    for owner_block in (block, block + 1 - 2 * lax.rem(block, 2)):
        total = add_rows(total, owner_block)
    own[...] = total

    is_client = (block == CLIENT) & (lax.rem(me, 2) == 0)
    is_pool = (block == POOL) & (lax.rem(me, 2) == 0)

    @pl.when(is_client)
    def _():
        pltpu.make_async_copy(partial_in, partial_in, partial_sem.at[1]).wait()
        project(own[...] + partial_in[...])
        for copy in code_copies():
            copy.wait_send()

    @pl.when(jnp.logical_not(is_client))
    def _():
        total = own[...]
        for owner_block in (2 - block // 2, 3 - 3 * (block // 2)):
            total = add_rows(total, owner_block)
        project(total)

    @pl.when(is_pool)
    def _():
        partial_copy.wait_send()

    for peer in range(n):

        @pl.when(peer != me)
        def _():
            ask_copy(peer).wait_send()

        kept = peer + (POOL - CLIENT) * quarter if pooled(peer, quarter) else peer

        @pl.when((peer != me) & (kept != me))
        def _():
            reply_copy(peer).wait_send()

    for other in range(reps):

        @pl.when(other != rep)
        def _():
            share_copy(other).wait_send()


def local(n, reps, features, seed_self, hub_ids, requests, counts, neighbors, weight, out_bias):
    rows, width = features.shape
    cap = requests.shape[1]
    hub_dev = hub_ids.shape[0]
    seeds, fanout = neighbors.shape
    quarter = n // 4
    hbm = pl.BlockSpec(memory_space=pltpu.HBM)
    dma = pltpu.SemaphoreType.DMA
    product = pl.pallas_call(
        functools.partial(kernel, n, reps),
        out_shape=pltpu.VMEM((seeds, width), jnp.float32),
        in_specs=[hbm] * 7,
        out_specs=pl.BlockSpec(memory_space=pltpu.VMEM),
        scratch_shapes=[
            pltpu.VMEM((rows, width), jnp.float32),
            pltpu.VMEM((seeds, width), jnp.float32),
            pltpu.VMEM(weight.shape, jnp.float32),
            pltpu.VMEM((1, hub_dev), jnp.int32),
            pltpu.VMEM((n, cap), jnp.int32),
            pltpu.VMEM((1, n), jnp.int32),
            pltpu.VMEM((fanout, seeds), jnp.int32),
            pltpu.VMEM((n, 1, LANES), jnp.int32),
            pltpu.VMEM((n, 1, LANES), jnp.int32),
            pltpu.VMEM((n, cap, width), jnp.float32),
            pltpu.VMEM((n, cap, width), jnp.float32),
            pltpu.VMEM((reps, hub_dev, width), jnp.float32),
            pltpu.VMEM((4, seeds, quarter * cap), jnp.bfloat16),
            pltpu.VMEM((2 * quarter, cap, width), jnp.float32),
            pltpu.VMEM((fanout, seeds), jnp.int32),
            pltpu.VMEM((1, n), jnp.int32),
            pltpu.VMEM((seeds, width), jnp.float32),
            pltpu.VMEM((seeds, width), jnp.float32),
            dma((7,)),
            dma((n,)),
            dma((n,)),
            dma((n,)),
            dma((n,)),
            dma((reps,)),
            dma((reps,)),
            pltpu.SemaphoreType.REGULAR((n,)),
            pltpu.SemaphoreType.REGULAR((reps,)),
            dma((2 * quarter,)),
            dma((2,)),
            dma((2,)),
            dma((2,)),
        ],
        compiler_params=pltpu.CompilerParams(collective_id=0, has_side_effects=True),
    )(features, seed_self, hub_ids[None], requests, counts[None], neighbors.T, weight)
    return jnp.maximum(product + out_bias, 0.0)


def solution(mesh):
    return jax.shard_map(
        functools.partial(local, mesh.shape["shard"], mesh.shape["rep"]),
        mesh=mesh,
        in_specs=(
            P(("rep", "shard"), None),
            P(("rep", "shard"), None),
            P(("rep", "shard")),
            P(("rep", "shard"), None),
            P(("rep", "shard")),
            P(("rep", "shard"), None),
            P(),
            P(),
        ),
        out_specs=P(("rep", "shard"), None),
        check_vma=False,
    )
```

time: 21.2 us -> 20.6 us (0.972)
  the two profiles are of different devices: /device:TPU:16 before, /device:TPU:10 now
where the time goes in v2:
time: 20.6 us; the launch traced here: 20.5 us
  Pallas kernels  19.8 us (96%)
  other arithmetic  0.67 us (3%)
    pallas_call x1, Pallas kernels, local(): pl.pallas_call(functools.partial(kernel, n, reps), out_shape=pltpu.VMEM((...  19.8 us
    max x1, other arithmetic, local(): return jnp.maximum(product + out_bias, 0.0)  0.67 us

profile of v2, /device:TPU:10, one launch (start us, length us, event | category | flops | bytes accessed | tf_op | source)
XLA Modules:
  0.0 20.5 jit_solution(17074958666569918769)
XLA Ops:
  0.0 0.0 copy-start
  0.0 19.8 %shard_map.82 = f32[128,256]{1,0:T(8,128)S(1)} custom-call(f32[512,256]{1,0:T(8,128)} %feat_hbm.1, f32[128,256]{1,0:T(8,128)} %self_hbm.1, s32[1,128]{1,0:T(1,128)} %bitcast.4, s32[16,32]{1,0:T(8,128)} %req_hbm.1, s32[1,16]{1,0:T(1,128)} %bitcast.5, s32[15,128]{1,0:T(8,128)} %bitcast.3, f32[256,256]{1,0:T(8,128)} %weight_hbm.1), custom_call_target="tpu_custom_call" | custom-call | tf_op jit(solution)/shard_map/pallas_call | solution.py:428
  19.8 0.0 copy-done
  19.8 0.7 %add_maximum_fusion = f32[128,256]{1,0:T(8,128)} fusion(f32[128,256]{1,0:T(8,128)S(1)} %shard_map.82, f32[256]{0:T(256)S(1)} %copy-done), kind=kLoop, calls=%fused_computation | loop fusion | flops 65536 | bytes 263168 | tf_op jit(solution)/shard_map/max | solution.py:468
Async XLA Ops:
  0.0 19.8 %copy-start = (f32[256]{0:T(256)S(1)}, f32[256]{0:T(256)}, u32[]{:S(2)}) copy-start(f32[256]{0:T(256)} %param.15) | copy-start | bytes 3076

commit v3 on v2

--- a/solution.py
+++ b/solution.py
@@ -8,11 +8,13 @@
 from jax.sharding import PartitionSpec as P
 
 LANES = 128
-CLIENT, POOL, FEED = 1, 2, 3
-
-
-def pooled(peer, quarter):
-    return peer // quarter == CLIENT and peer % 2 == 0
+
+
+def pool_of(peer, quarter):
+    block = peer // quarter
+    if block in (1, 2) and peer % 2 == 0:
+        return peer + (3 - 2 * block) * quarter
+    return None
 
 
 def halves(values):
@@ -34,9 +36,9 @@
 
 def kernel(
     n, reps, feat_hbm, self_hbm, hub_hbm, req_hbm, cnt_hbm, nbr_hbm, weight_hbm, out_ref,
-    feat, own, weight, hub_ref, req_ref, cnt_ref, nbr_ref, table, req_recv, gathered, fetched, hubs, slot_tally,
+    feat, own, weight, hub_ref, req_ref, cnt_ref, nbr_ref, table, req_recv, high_ref, low_ref, gathered, fetched, hubs, slot_tally,
     pool, pool_codes, pool_counts, partial, partial_in,
-    local_sem, ask_sem, ask_recv_sem, row_send_sem, row_recv_sem, hub_send_sem, hub_recv_sem, present, rep_present,
+    local_sem, ask_sem, ask_recv_sem, row_send_sem, row_recv_sem, hub_send_sem, hub_recv_sem,
     pool_sem, code_send_sem, code_recv_sem, partial_sem,
 ):
     me = lax.axis_index("shard")
@@ -48,6 +50,12 @@
     hub_total = hub_dev * reps
     quarter = n // 4
     block, place = me // quarter, lax.rem(me, quarter)
+
+    barrier = pltpu.get_barrier_semaphore()
+    for off in range(1, n):
+        pl.semaphore_signal(barrier, inc=1, device_id={"shard": lax.rem(me + off, n)})
+    for off in range(1, reps):
+        pl.semaphore_signal(barrier, inc=1, device_id={"rep": lax.rem(rep + off, reps)})
 
     loads = [
         pltpu.make_async_copy(src, dst, local_sem.at[i])
@@ -66,38 +74,28 @@
     for load in loads:
         load.start()
 
-    barrier = pltpu.get_barrier_semaphore()
-
-    def greet(peer, carry):
-        pl.semaphore_signal(barrier, inc=1, device_id={"shard": peer})
-        return carry
-
-    lax.fori_loop(me + 1, n, greet, 0)
-    for other in range(1, reps):
-
-        @pl.when(other > rep)
-        def _():
-            pl.semaphore_signal(barrier, inc=1, device_id={"rep": other})
-
-    @pl.when(me + rep > 0)
-    def _():
-        pl.semaphore_wait(barrier, me + rep)
-
-    def tell(peer, carry):
-        pl.semaphore_signal(present.at[me], inc=1, device_id={"shard": peer})
-        return carry
-
-    lax.fori_loop(0, me, tell, 0)
-    for other in range(reps - 1):
-
-        @pl.when(other < rep)
-        def _():
-            pl.semaphore_signal(rep_present.at[rep], inc=1, device_id={"rep": other})
-
     loads[0].wait()
     lists = jnp.concatenate([req_ref[...], jnp.zeros((n, LANES - cap), jnp.int32)], axis=1)
     table[...] = lists.reshape(n, 1, LANES)
     req_recv[me] = table[me]
+
+    row_iota = lax.broadcasted_iota(jnp.int32, (LANES, rows), 1)
+
+    def split():
+        loads[1].wait()
+        high_ref[...], low_ref[...] = halves(feat[...])
+
+    def gather(pick):
+        pick = pick.astype(jnp.float32).astype(jnp.bfloat16)
+        return dot(pick, high_ref[...]) + dot(pick, low_ref[...])
+
+    def gather_hubs():
+        loads[2].wait()
+        hub_columns = columns_of(jnp.broadcast_to(hub_ref[...], (8, hub_dev)))
+        hubs[rep] = gather(hub_columns[:, 0:1] == row_iota)
+
+    def enter():
+        pl.semaphore_wait(barrier, n - 1 + reps - 1)
 
     loads[3].wait()
     loads[4].wait()
@@ -114,22 +112,16 @@
     def ask(own_block, to_block):
         for spot in (*range(1, quarter, 2), *range(0, quarter, 2)):
             peer = to_block * quarter + spot
-            if to_block > own_block:
-                pl.semaphore_wait(present.at[peer], 1)
             if to_block != own_block:
                 ask_copy(peer).start()
                 continue
 
-            @pl.when(spot > place)
-            def _():
-                pl.semaphore_wait(present.at[peer], 1)
-
             @pl.when(spot != place)
             def _():
                 ask_copy(peer).start()
 
     def code_copies():
-        peer = POOL * quarter + place
+        peer = (3 - block) * quarter + place
         return [
             pltpu.make_async_remote_copy(
                 src_ref=src,
@@ -145,22 +137,6 @@
         for copy in code_copies():
             copy.start()
 
-    for b in range(1, 4):
-
-        @pl.when(block == b)
-        def _():
-            for to_block in range(b):
-                ask(b, to_block)
-
-    loads[1].wait()
-    high, low = halves(feat[...])
-    row_iota = lax.broadcasted_iota(jnp.int32, (LANES, rows), 1)
-
-    loads[2].wait()
-    hub_columns = columns_of(jnp.broadcast_to(hub_ref[...], (8, hub_dev)))
-    pick = (hub_columns[:, 0:1] == row_iota).astype(jnp.float32).astype(jnp.bfloat16)
-    hubs[rep] = dot(pick, high) + dot(pick, low)
-
     def share_copy(other):
         return pltpu.make_async_remote_copy(
             src_ref=hubs.at[rep],
@@ -173,10 +149,6 @@
     def share():
         for other in range(reps):
 
-            @pl.when(other > rep)
-            def _():
-                pl.semaphore_wait(rep_present.at[other], 1)
-
             @pl.when(other != rep)
             def _():
                 share_copy(other).start()
@@ -207,28 +179,30 @@
         request_columns = columns_of(jnp.concatenate([req_recv[peer] for peer in peers], axis=0))
         for first in range(0, len(peers), batch):
             group = peers[first : first + batch]
-            pick = jnp.concatenate(
-                [
-                    (request_columns[:cap, i : i + 1] == row_iota[:cap]).astype(jnp.float32)
-                    for i in range(first, first + len(group))
-                ],
-                axis=0,
-            ).astype(jnp.bfloat16)
-            picked = dot(pick, high) + dot(pick, low)
+            picked = gather(
+                jnp.concatenate(
+                    [
+                        request_columns[:cap, i : i + 1] == row_iota[:cap]
+                        for i in range(first, first + len(group))
+                    ],
+                    axis=0,
+                )
+            )
             for i, peer in enumerate(group):
                 gathered[peer] = picked[i * cap : (i + 1) * cap]
             for peer in group:
-                if own_block in (POOL, FEED) and pooled(peer, quarter):
-                    row = place + (quarter if own_block == FEED else 0)
+                pool_peer = pool_of(peer, quarter)
+                if pool_peer is not None and own_block // 2 != peer_block // 2:
+                    row = lax.rem(me, 2 * quarter)
                     forward = pltpu.make_async_remote_copy(
                         src_ref=gathered.at[peer],
                         dst_ref=pool.at[row],
                         send_sem=row_send_sem.at[peer],
                         recv_sem=pool_sem.at[row],
-                        device_id={"shard": peer + (POOL - CLIENT) * quarter},
+                        device_id={"shard": pool_peer},
                     )
-                    if own_block == POOL:
-                        pl.when(peer + (POOL - CLIENT) * quarter != me)(forward.start)
+                    if own_block == 3 - peer_block:
+                        pl.when(pool_peer != me)(forward.start)
                     else:
                         forward.start()
                 else:
@@ -255,23 +229,24 @@
         dst_ref=partial_in,
         send_sem=partial_sem.at[0],
         recv_sem=partial_sem.at[1],
-        device_id={"shard": CLIENT * quarter + place},
+        device_id={"shard": (3 - block) * quarter + place},
     )
 
-    def pool_rows():
+    def pool_rows(own_block):
         for i, ref in enumerate((pool_codes, pool_counts)):
             pltpu.make_async_copy(ref, ref, code_recv_sem.at[i]).wait()
-        low = POOL * quarter * cap
+        low = own_block // 2 * 2 * quarter * cap
         part = quarter * cap
         counted = tally_of(columns_of(pool_codes[...]), hub_total + low, 2 * part)
         counted = (counted * live_of(pool_counts[...], low, 2 * part)).astype(jnp.bfloat16)
-        pool[place] = gathered[CLIENT * quarter + place]
+        pool[lax.rem(me, 2 * quarter)] = gathered[(3 - own_block) * quarter + place]
         total = None
-        for i in range(2):
+        own_part = own_block % 2
+        for i in (own_part, 1 - own_part):
             for spot in range(quarter):
                 row = i * quarter + spot
                 arrival = pltpu.make_async_copy(pool.at[row], pool.at[row], pool_sem.at[row])
-                if i == 0:
+                if i == own_part:
                     pl.when(spot != place)(arrival.wait)
                 else:
                     arrival.wait()
@@ -286,52 +261,71 @@
     front, back = range(quarter // 2), range(quarter // 2, quarter)
     @pl.when(block == 0)
     def _():
+        split()
+        gather_hubs()
+        enter()
+        ask(0, 3)
+        ask(0, 2)
+        ask(0, 1)
         ask(0, 0)
-        ask(0, 1)
-        ask(0, 2)
-        ask(0, 3)
         share()
-        answer(0, 1, odd)
+        answer(0, 2, even)
         answer(0, 0, every)
-        answer(0, 1, even)
-        answer(0, 2, every)
         answer(0, 3, every)
+        answer(0, 1, every)
+        answer(0, 2, odd)
 
     @pl.when(block == 1)
     def _():
-        share()
-        ask(1, 1)
+        split()
+        gather_hubs()
+        enter()
+        ask(1, 3)
+        ask(1, 0)
         ask(1, 2)
         pl.when(lax.rem(me, 2) == 0)(send_codes)
-        ask(1, 3)
+        ask(1, 1)
         answer(1, 2, odd)
         answer(1, 0, every)
         answer(1, 2, even)
+        share()
         answer(1, 3, every)
         answer(1, 1, every)
+        pl.when(lax.rem(me, 2) == 0)(functools.partial(pool_rows, 1))
 
     @pl.when(block == 2)
     def _():
+        split()
+        enter()
+        ask(2, 0)
+        ask(2, 1)
+        pl.when(lax.rem(me, 2) == 0)(send_codes)
         ask(2, 2)
         ask(2, 3)
+        gather_hubs()
         share()
         answer(2, 1, odd)
         answer(2, 1, even)
         answer(2, 0, every)
         answer(2, 2, every)
         answer(2, 3, every)
-        pl.when(lax.rem(me, 2) == 0)(pool_rows)
+        pl.when(lax.rem(me, 2) == 0)(functools.partial(pool_rows, 2))
 
     @pl.when(block == 3)
     def _():
-        share()
+        enter()
+        ask(3, 0)
+        ask(3, 1)
+        ask(3, 2)
         ask(3, 3)
+        split()
+        gather_hubs()
         answer(3, 3, every)
         answer(3, 1, even)
-        answer(3, 2, odd)
+        answer(3, 1, odd)
+        share()
         answer(3, 0, every)
-        answer(3, 1, odd)
-        answer(3, 2, even)
+        answer(3, 2, every)
 
     fetched[me] = gathered[me]
 
@@ -377,14 +371,13 @@
         total = add_rows(total, owner_block)
     own[...] = total
 
-    is_client = (block == CLIENT) & (lax.rem(me, 2) == 0)
-    is_pool = (block == POOL) & (lax.rem(me, 2) == 0)
+    is_client = ((block == 1) | (block == 2)) & (lax.rem(me, 2) == 0)
 
     @pl.when(is_client)
     def _():
         pltpu.make_async_copy(partial_in, partial_in, partial_sem.at[1]).wait()
         project(own[...] + partial_in[...])
-        for copy in code_copies():
+        for copy in (*code_copies(), partial_copy):
             copy.wait_send()
 
     @pl.when(jnp.logical_not(is_client))
@@ -394,17 +387,14 @@
             total = add_rows(total, owner_block)
         project(total)
 
-    @pl.when(is_pool)
-    def _():
-        partial_copy.wait_send()
-
     for peer in range(n):
 
         @pl.when(peer != me)
         def _():
             ask_copy(peer).wait_send()
 
-        kept = peer + (POOL - CLIENT) * quarter if pooled(peer, quarter) else peer
+        pool_peer = pool_of(peer, quarter)
+        kept = peer if pool_peer is None else pool_peer
 
         @pl.when((peer != me) & (kept != me))
         def _():
@@ -440,6 +430,8 @@
             pltpu.VMEM((fanout, seeds), jnp.int32),
             pltpu.VMEM((n, 1, LANES), jnp.int32),
             pltpu.VMEM((n, 1, LANES), jnp.int32),
+            pltpu.VMEM((rows, width), jnp.bfloat16),
+            pltpu.VMEM((rows, width), jnp.bfloat16),
             pltpu.VMEM((n, cap, width), jnp.float32),
             pltpu.VMEM((n, cap, width), jnp.float32),
             pltpu.VMEM((reps, hub_dev, width), jnp.float32),
@@ -456,8 +448,6 @@
             dma((n,)),
             dma((reps,)),
             dma((reps,)),
-            pltpu.SemaphoreType.REGULAR((n,)),
-            pltpu.SemaphoreType.REGULAR((reps,)),
             dma((2 * quarter,)),
             dma((2,)),
             dma((2,)),

time: 20.6 us -> 20.3 us (0.985)
  the two profiles are of different devices: /device:TPU:10 before, /device:TPU:1 now
where the time goes in v3:
time: 20.3 us; the launch traced here: 20.1 us
  Pallas kernels  19.4 us (96%)
  other arithmetic  0.67 us (3%)
    pallas_call x1, Pallas kernels, local(): pl.pallas_call(functools.partial(kernel, n, reps), out_shape=pltpu.VMEM((...  19.4 us
    max x1, other arithmetic, local(): return jnp.maximum(product + out_bias, 0.0)  0.67 us

profile of v3, /device:TPU:1, one launch (start us, length us, event | category | flops | bytes accessed | tf_op | source)
XLA Modules:
  0.0 20.1 jit_solution(2210711378889147675)
XLA Ops:
  0.0 0.0 copy-start
  0.0 19.4 %shard_map.82 = f32[128,256]{1,0:T(8,128)S(1)} custom-call(f32[512,256]{1,0:T(8,128)} %feat_hbm.1, f32[128,256]{1,0:T(8,128)} %self_hbm.1, s32[1,128]{1,0:T(1,128)} %bitcast.4, s32[16,32]{1,0:T(8,128)} %req_hbm.1, s32[1,16]{1,0:T(1,128)} %bitcast.5, s32[15,128]{1,0:T(8,128)} %bitcast.3, f32[256,256]{1,0:T(8,128)} %weight_hbm.1), custom_call_target="tpu_custom_call" | custom-call | tf_op jit(solution)/shard_map/pallas_call | solution.py:418
  19.4 0.0 copy-done
  19.5 0.7 %add_maximum_fusion = f32[128,256]{1,0:T(8,128)} fusion(f32[128,256]{1,0:T(8,128)S(1)} %shard_map.82, f32[256]{0:T(256)S(1)} %copy-done), kind=kLoop, calls=%fused_computation | loop fusion | flops 65536 | bytes 263168 | tf_op jit(solution)/shard_map/max | solution.py:458
Async XLA Ops:
  0.0 19.4 %copy-start = (f32[256]{0:T(256)S(1)}, f32[256]{0:T(256)}, u32[]{:S(2)}) copy-start(f32[256]{0:T(256)} %param.15) | copy-start | bytes 3076

commit v4 on v3

--- a/solution.py
+++ b/solution.py
@@ -38,8 +38,7 @@
     n, reps, feat_hbm, self_hbm, hub_hbm, req_hbm, cnt_hbm, nbr_hbm, weight_hbm, out_ref,
     feat, own, weight, hub_ref, req_ref, cnt_ref, nbr_ref, table, req_recv, high_ref, low_ref, gathered, fetched, hubs, slot_tally,
     pool, pool_codes, pool_counts, partial, partial_in,
-    local_sem, ask_sem, ask_recv_sem, row_send_sem, row_recv_sem, hub_send_sem, hub_recv_sem,
-    pool_sem, code_send_sem, code_recv_sem, partial_sem,
+    local_sem, ask_recv_sem, row_recv_sem, hub_recv_sem, pool_sem, code_recv_sem, partial_sem,
 ):
     me = lax.axis_index("shard")
     rep = lax.axis_index("rep")
@@ -82,7 +81,8 @@
     row_iota = lax.broadcasted_iota(jnp.int32, (LANES, rows), 1)
 
     def split():
-        loads[1].wait()
+        for load in (loads[1], loads[5], loads[6]):
+            load.wait()
         high_ref[...], low_ref[...] = halves(feat[...])
 
     def gather(pick):
@@ -104,8 +104,8 @@
         return pltpu.make_async_remote_copy(
             src_ref=table.at[peer],
             dst_ref=req_recv.at[me],
-            send_sem=ask_sem.at[peer],
-            recv_sem=ask_recv_sem.at[me],
+            send_sem=local_sem.at[0],
+            recv_sem=ask_recv_sem.at[2 * block + lax.rem(me, 2)],
             device_id={"shard": peer},
         )
 
@@ -126,7 +126,7 @@
             pltpu.make_async_remote_copy(
                 src_ref=src,
                 dst_ref=dst,
-                send_sem=code_send_sem.at[i],
+                send_sem=local_sem.at[3 + i],
                 recv_sem=code_recv_sem.at[i],
                 device_id={"shard": peer},
             )
@@ -141,8 +141,8 @@
         return pltpu.make_async_remote_copy(
             src_ref=hubs.at[rep],
             dst_ref=hubs.at[rep],
-            send_sem=hub_send_sem.at[other],
-            recv_sem=hub_recv_sem.at[rep],
+            send_sem=local_sem.at[2],
+            recv_sem=hub_recv_sem.at[0],
             device_id={"rep": other},
         )
 
@@ -152,6 +152,10 @@
             @pl.when(other != rep)
             def _():
                 share_copy(other).start()
+
+    def take(buffer, count, sem):
+        part = buffer.at[pl.ds(0, count)]
+        pltpu.make_async_copy(part, part, sem).wait()
 
     batch = min(LANES // cap, quarter)
 
@@ -159,8 +163,8 @@
         return pltpu.make_async_remote_copy(
             src_ref=gathered.at[peer],
             dst_ref=fetched.at[me],
-            send_sem=row_send_sem.at[peer],
-            recv_sem=row_recv_sem.at[me],
+            send_sem=local_sem.at[1],
+            recv_sem=row_recv_sem.at[block],
             device_id={"shard": peer},
         )
 
@@ -173,9 +177,21 @@
             else:
                 action()
 
-        for peer in peers:
-            ref = req_recv.at[peer]
-            unless_me(peer, pltpu.make_async_copy(ref, ref, ask_recv_sem.at[peer]).wait)
+        for parity in sorted({spot % 2 for spot in places}):
+            sem = ask_recv_sem.at[2 * peer_block + parity]
+            count = quarter // 2
+            if peer_block != own_block:
+                take(req_recv, count, sem)
+                continue
+
+            @pl.when(lax.rem(me, 2) == parity)
+            def _():
+                take(req_recv, count - 1, sem)
+
+            @pl.when(lax.rem(me, 2) != parity)
+            def _():
+                take(req_recv, count, sem)
+
         request_columns = columns_of(jnp.concatenate([req_recv[peer] for peer in peers], axis=0))
         for first in range(0, len(peers), batch):
             group = peers[first : first + batch]
@@ -197,8 +213,8 @@
                     forward = pltpu.make_async_remote_copy(
                         src_ref=gathered.at[peer],
                         dst_ref=pool.at[row],
-                        send_sem=row_send_sem.at[peer],
-                        recv_sem=pool_sem.at[row],
+                        send_sem=local_sem.at[1],
+                        recv_sem=pool_sem.at[lax.rem(block, 2)],
                         device_id={"shard": pool_peer},
                     )
                     if own_block == 3 - peer_block:
@@ -227,8 +243,8 @@
     partial_copy = pltpu.make_async_remote_copy(
         src_ref=partial,
         dst_ref=partial_in,
-        send_sem=partial_sem.at[0],
-        recv_sem=partial_sem.at[1],
+        send_sem=local_sem.at[5],
+        recv_sem=partial_sem.at[0],
         device_id={"shard": (3 - block) * quarter + place},
     )
 
@@ -243,13 +259,7 @@
         total = None
         own_part = own_block % 2
         for i in (own_part, 1 - own_part):
-            for spot in range(quarter):
-                row = i * quarter + spot
-                arrival = pltpu.make_async_copy(pool.at[row], pool.at[row], pool_sem.at[row])
-                if i == own_part:
-                    pl.when(spot != place)(arrival.wait)
-                else:
-                    arrival.wait()
+            take(pool, quarter - 1 if i == own_part else quarter, pool_sem.at[i])
             row_high, row_low = halves(pool[i * quarter : (i + 1) * quarter].reshape(part, width))
             chosen = counted[:, i * part : (i + 1) * part]
             term = dot(chosen, row_high) + dot(chosen, row_low)
@@ -339,26 +349,16 @@
     for b in range(4):
         slot_tally[b] = live_tally[:, b * quarter * cap : (b + 1) * quarter * cap].astype(jnp.bfloat16)
 
-    loads[5].wait()
-    for other in range(reps):
-
-        @pl.when(other != rep)
-        def _():
-            pltpu.make_async_copy(hubs.at[other], hubs.at[other], hub_recv_sem.at[other]).wait()
-
+    take(table, n - 1, local_sem.at[0])
+    if reps > 1:
+        take(hubs, reps - 1, local_sem.at[2])
+        take(hubs, reps - 1, hub_recv_sem.at[0])
     hub_high, hub_low = halves(hubs[...].reshape(hub_total, width))
     total = own[...] + (dot(hub_tally, hub_high) + dot(hub_tally, hub_low))
-    loads[6].wait()
     weight_high, weight_low = halves(weight[...])
 
-    def add_rows(total, owner_block):
-        for spot in range(quarter):
-            owner = owner_block * quarter + spot
-
-            @pl.when(owner != me)
-            def _():
-                pltpu.make_async_copy(fetched.at[owner], fetched.at[owner], row_recv_sem.at[owner]).wait()
-
+    def add_rows(total, owner_block, count):
+        take(fetched, count, row_recv_sem.at[owner_block])
         row_high, row_low = halves(fetched[pl.ds(owner_block * quarter, quarter)].reshape(quarter * cap, width))
         counted = slot_tally[owner_block]
         return total + (dot(counted, row_high) + dot(counted, row_low))
@@ -367,44 +367,26 @@
         mean_high, mean_low = halves(total * scale)
         out_ref[...] = dot(mean_high, weight_high) + (dot(mean_high, weight_low) + dot(mean_low, weight_high))
 
-    for owner_block in (block, block + 1 - 2 * lax.rem(block, 2)):
-        total = add_rows(total, owner_block)
-    own[...] = total
+    total = add_rows(total, block, quarter - 1)
+    own[...] = add_rows(total, block + 1 - 2 * lax.rem(block, 2), quarter)
 
     is_client = ((block == 1) | (block == 2)) & (lax.rem(me, 2) == 0)
 
     @pl.when(is_client)
     def _():
-        pltpu.make_async_copy(partial_in, partial_in, partial_sem.at[1]).wait()
-        project(own[...] + partial_in[...])
+        take(gathered, n - 2, local_sem.at[1])
         for copy in (*code_copies(), partial_copy):
             copy.wait_send()
+        pltpu.make_async_copy(partial_in, partial_in, partial_sem.at[0]).wait()
+        project(own[...] + partial_in[...])
 
     @pl.when(jnp.logical_not(is_client))
     def _():
+        take(gathered, n - 1, local_sem.at[1])
         total = own[...]
         for owner_block in (2 - block // 2, 3 - 3 * (block // 2)):
-            total = add_rows(total, owner_block)
+            total = add_rows(total, owner_block, quarter)
         project(total)
-
-    for peer in range(n):
-
-        @pl.when(peer != me)
-        def _():
-            ask_copy(peer).wait_send()
-
-        pool_peer = pool_of(peer, quarter)
-        kept = peer if pool_peer is None else pool_peer
-
-        @pl.when((peer != me) & (kept != me))
-        def _():
-            reply_copy(peer).wait_send()
-
-    for other in range(reps):
-
-        @pl.when(other != rep)
-        def _():
-            share_copy(other).wait_send()
 
 
 def local(n, reps, features, seed_self, hub_ids, requests, counts, neighbors, weight, out_bias):
@@ -442,16 +424,12 @@
             pltpu.VMEM((seeds, width), jnp.float32),
             pltpu.VMEM((seeds, width), jnp.float32),
             dma((7,)),
-            dma((n,)),
-            dma((n,)),
-            dma((n,)),
-            dma((n,)),
-            dma((reps,)),
-            dma((reps,)),
-            dma((2 * quarter,)),
+            dma((8,)),
+            dma((4,)),
+            dma((1,)),
             dma((2,)),
             dma((2,)),
-            dma((2,)),
+            dma((1,)),
         ],
         compiler_params=pltpu.CompilerParams(collective_id=0, has_side_effects=True),
     )(features, seed_self, hub_ids[None], requests, counts[None], neighbors.T, weight)

time: 20.3 us -> 19.7 us (0.970)
  Pallas kernels: 19.4 us -> 18.8 us
    pallas_call x1, Pallas kernels: 19.4 us -> 18.8 us  [local(): pl.pallas_call(functools.partial(kernel, n, reps), out_shape=pltpu.VMEM((...]
where the time goes in v4:
time: 19.7 us; the launch traced here: 19.5 us
  Pallas kernels  18.8 us (95%)
  other arithmetic  0.67 us (3%)
    pallas_call x1, Pallas kernels, local(): pl.pallas_call(functools.partial(kernel, n, reps), out_shape=pltpu.VMEM((...  18.8 us
    max x1, other arithmetic, local(): return jnp.maximum(product + out_bias, 0.0)  0.67 us

profile of v4, /device:TPU:1, one launch (start us, length us, event | category | flops | bytes accessed | tf_op | source)
XLA Modules:
  0.0 19.5 jit_solution(6179959859375807890)
XLA Ops:
  0.0 0.0 copy-start
  0.0 18.8 %shard_map.82 = f32[128,256]{1,0:T(8,128)S(1)} custom-call(f32[512,256]{1,0:T(8,128)} %feat_hbm.1, f32[128,256]{1,0:T(8,128)} %self_hbm.1, s32[1,128]{1,0:T(1,128)} %bitcast.4, s32[16,32]{1,0:T(8,128)} %req_hbm.1, s32[1,16]{1,0:T(1,128)} %bitcast.5, s32[15,128]{1,0:T(8,128)} %bitcast.3, f32[256,256]{1,0:T(8,128)} %weight_hbm.1), custom_call_target="tpu_custom_call" | custom-call | tf_op jit(solution)/shard_map/pallas_call | solution.py:400
  18.8 0.0 copy-done
  18.8 0.7 %add_maximum_fusion = f32[128,256]{1,0:T(8,128)} fusion(f32[128,256]{1,0:T(8,128)S(1)} %shard_map.82, f32[256]{0:T(256)S(1)} %copy-done), kind=kLoop, calls=%fused_computation | loop fusion | flops 65536 | bytes 263168 | tf_op jit(solution)/shard_map/max | solution.py:436
Async XLA Ops:
  0.0 18.8 %copy-start = (f32[256]{0:T(256)S(1)}, f32[256]{0:T(256)}, u32[]{:S(2)}) copy-start(f32[256]{0:T(256)} %param.15) | copy-start | bytes 3076

commit v5 on v4

--- a/solution.py
+++ b/solution.py
@@ -361,7 +361,7 @@
         take(fetched, count, row_recv_sem.at[owner_block])
         row_high, row_low = halves(fetched[pl.ds(owner_block * quarter, quarter)].reshape(quarter * cap, width))
         counted = slot_tally[owner_block]
-        return total + (dot(counted, row_high) + dot(counted, row_low))
+        return total + dot(jnp.concatenate([counted] * 2, axis=1), jnp.concatenate([row_high, row_low], axis=0))
 
     def project(total):
         mean_high, mean_low = halves(total * scale)
@@ -384,7 +384,7 @@
     def _():
         take(gathered, n - 1, local_sem.at[1])
         total = own[...]
-        for owner_block in (2 - block // 2, 3 - 3 * (block // 2)):
+        for owner_block in (3 - 3 * (block // 2), 2 - block // 2):
             total = add_rows(total, owner_block, quarter)
         project(total)
 

time: 19.7 us -> 19.5 us (0.990)
  no operation moved by 1% of the time
where the time goes in v5:
time: 19.5 us; the launch traced here: 19.4 us
  Pallas kernels  18.7 us (96%)
  other arithmetic  0.67 us (3%)
    pallas_call x1, Pallas kernels, local(): pl.pallas_call(functools.partial(kernel, n, reps), out_shape=pltpu.VMEM((...  18.7 us
    max x1, other arithmetic, local(): return jnp.maximum(product + out_bias, 0.0)  0.67 us

profile of v5, /device:TPU:1, one launch (start us, length us, event | category | flops | bytes accessed | tf_op | source)
XLA Modules:
  0.0 19.4 jit_solution(4859348889155591741)
XLA Ops:
  0.0 0.0 copy-start
  0.0 18.7 %shard_map.82 = f32[128,256]{1,0:T(8,128)S(1)} custom-call(f32[512,256]{1,0:T(8,128)} %feat_hbm.1, f32[128,256]{1,0:T(8,128)} %self_hbm.1, s32[1,128]{1,0:T(1,128)} %bitcast.4, s32[16,32]{1,0:T(8,128)} %req_hbm.1, s32[1,16]{1,0:T(1,128)} %bitcast.5, s32[15,128]{1,0:T(8,128)} %bitcast.3, f32[256,256]{1,0:T(8,128)} %weight_hbm.1), custom_call_target="tpu_custom_call" | custom-call | tf_op jit(solution)/shard_map/pallas_call | solution.py:400
  18.7 0.0 copy-done
  18.7 0.7 %add_maximum_fusion = f32[128,256]{1,0:T(8,128)} fusion(f32[128,256]{1,0:T(8,128)S(1)} %shard_map.82, f32[256]{0:T(256)S(1)} %copy-done), kind=kLoop, calls=%fused_computation | loop fusion | flops 65536 | bytes 263168 | tf_op jit(solution)/shard_map/max | solution.py:436
Async XLA Ops:
  0.0 18.7 %copy-start = (f32[256]{0:T(256)S(1)}, f32[256]{0:T(256)}, u32[]{:S(2)}) copy-start(f32[256]{0:T(256)} %param.15) | copy-start | bytes 3076
